TPU v7x, 256 devices: a whole 4x4x8 slice. The times are simulated.
256 devices in a mesh: row: 16 (over x, y_hi, core), col: 16 (over y_lo, z).
Axes of the slice: x: 4, y: 4 (y_hi: 2, y_lo: 2; y = y_hi * 2 + y_lo), z: 8, core: 2. Of those that a mesh axis runs over, the one named last changes fastest.
Arguments:
- expression: bfloat16 [32768, 1024], P(('row', 'col')), may hold values from -200 to 200, as said below
- powers: int32 [10], replicated, may hold values from 1 to 20
Outputs:
- log_degree: float32 [10, 32768], P(None, ('row', 'col'))
- degree_freq: float32 [10, 10], replicated
- fit_slope: float32 [10], replicated
- mean_log: float32 [10], replicated
Inputs may be any that keep to these rules, and one draw needn't show every extreme that they name: Finite expression values.
All inputs are finite; a program needn't handle non-finite values.
Results may differ from a plain program's by a relative error of at most 0.0003.
Values may be sent and summed in bfloat16 or wider, within the bound.
A program may use at most 64 MiB of HBM per device.

v0:
```python
import functools

import jax
import jax.numpy as jnp
from jax import lax
from jax.sharding import Mesh
from jax.sharding import PartitionSpec as P

BINS = 10
COL = ("col_0", "col_1")
ROW = ("row_0", "row_1", "row_2")
ROW_COL = ("row_0", "row_1", "row_2", "col_0", "col_1")


def joined_along(blocks, dim):
    blocks = jnp.moveaxis(blocks, 0, dim)
    dims = blocks.shape
    return blocks.reshape(*dims[:dim], dims[dim] * dims[dim + 1], *dims[dim + 2 :])


def stacked_from(shard, axes, turns):
    blocks = shard[None]
    for k in turns:
        blocks = lax.all_gather(blocks, axes[k], axis=0, tiled=True)
    carried = [lax.axis_size(axes[k]) for k in reversed(turns)]
    blocks = blocks.reshape(*carried, *shard.shape)
    turned = sorted(range(len(turns)), key=lambda place: turns[len(turns) - 1 - place])
    return blocks.transpose(*turned, *range(len(turns), blocks.ndim)).reshape(-1, *shard.shape)


def gathered_by_axis(shard, axes, turns, dim):
    return joined_along(stacked_from(shard, axes, turns), dim)


def copy_for_each(shard, axis):
    size = lax.axis_size(axis)
    return lax.all_to_all(
        jnp.broadcast_to(shard[None], (size, *shard.shape)), axis, 0, 0, tiled=True
    )


def gathered_by_axis_2(shard, axes, dim):
    far, near = axes
    blocks = copy_for_each(copy_for_each(shard, far), near)
    return joined_along(blocks.swapaxes(0, 1).reshape(-1, *shard.shape), dim)


def split_up(shard, dim, size):
    before, after = (shard.shape[:dim], shard.shape[dim + 1 :])
    return jnp.moveaxis(shard.reshape(*before, size, -1, *after), dim, 0)


def summed_on_arrival(shard, axis, dim):
    blocks = split_up(shard, dim, lax.axis_size(axis))
    arrived = lax.all_to_all(blocks, axis, split_axis=0, concat_axis=0, tiled=True)
    return arrived.sum(axis=0)


def over_axes(shard, axes):
    return functools.reduce(lax.pmax, axes, shard)


def over_axes_2(shard, axes):
    return functools.reduce(lax.psum, axes, shard)


def gene_stats(genes):
    values = genes.astype(jnp.float32)
    gene_mean = jnp.mean(values, axis=1)
    centred = values - gene_mean[:, None]
    gene_inv = lax.rsqrt(jnp.mean(centred * centred, axis=1) + 1e-06)
    return (gene_mean, gene_inv)


def add_slice(totals, addend, start):
    current = lax.dynamic_slice_in_dim(totals, start, addend.shape[1], 1)
    return lax.dynamic_update_slice_in_dim(totals, current + addend, start, 1)


def block_sums(left_genes, right_genes, exponents, row_list, carry, left_start):
    row_count = left_genes.shape[0]
    block_rows = 256
    samples = left_genes.shape[1]
    left_mean, left_inv = gene_stats(left_genes)
    right_mean, right_inv = gene_stats(right_genes)

    def one_block(block_index, totals):
        row_totals, column_totals = totals
        offset = block_index * block_rows
        row_block = lax.dynamic_slice_in_dim(left_genes, offset, block_rows, 0)
        block_mean = lax.dynamic_slice_in_dim(left_mean, offset, block_rows, 0)
        block_inv = lax.dynamic_slice_in_dim(left_inv, offset, block_rows, 0)
        raw = lax.dot_general(
            row_block, right_genes, (((1,), (1,)), ((), ())), preferred_element_type=jnp.float32
        )
        pearson = (
            (raw / samples - block_mean[:, None] * right_mean[None, :])
            * block_inv[:, None]
            * right_inv[None, :]
        )
        log_abs = jnp.log(jnp.abs(pearson))
        row_parts = []
        for power_index in row_list:
            row_parts.append(jnp.sum(jnp.exp(exponents[power_index] * log_abs), axis=1))
        if row_parts:
            row_totals = add_slice(row_totals, jnp.stack(row_parts), left_start + offset)
        return (row_totals, column_totals)

    return lax.fori_loop(0, row_count // block_rows, one_block, carry)


def on_device(expression, powers):
    exponents = powers.astype(jnp.float32)
    npower = powers.shape[0]
    local_genes = expression.shape[0]
    row_width = local_genes * lax.axis_size(COL)
    column_width = local_genes * lax.axis_size(ROW)
    row_list = list(range(npower))
    col_list = []
    initial = (
        jnp.zeros((len(row_list), row_width), jnp.float32),
        jnp.zeros((max(len(col_list), 1), column_width), jnp.float32),
    )
    left_genes = gathered_by_axis(expression, COL, (0, 1), 0)
    row_totals, column_totals = block_sums(
        left_genes,
        gathered_by_axis_2(expression, (("row_0", "row_1"), "row_2"), 0),
        exponents,
        row_list,
        initial,
        0,
    )
    degree = summed_on_arrival(row_totals, COL, 1)
    peak = over_axes(jnp.max(degree, axis=1), ROW_COL)
    position = jnp.clip(BINS * degree / peak[:, None] - 0.5, 0.0, BINS - 1.0)
    centres = jnp.arange(BINS, dtype=jnp.float32)
    weights = jnp.maximum(0.0, 1.0 - jnp.abs(position[:, :, None] - centres[None, None, :]))
    freq_total, degree_total = (
        over_axes_2(jnp.sum(weights, axis=1), ROW_COL),
        over_axes_2(jnp.sum(degree, axis=1), ROW_COL),
    )
    genes_all = local_genes * lax.axis_size(ROW) * lax.axis_size(COL)
    degree_freq = freq_total / genes_all
    mean_log = jnp.log10(degree_total / genes_all)
    xfit = jnp.log10((centres[None, :] + 0.5) * peak[:, None] / BINS)
    yfit = jnp.log10(degree_freq + 1.0 / genes_all)
    xdev = xfit - jnp.mean(xfit, axis=1, keepdims=True)
    ydev = yfit - jnp.mean(yfit, axis=1, keepdims=True)
    fit_slope = jnp.sum(xdev * ydev, axis=1) / jnp.sum(xdev * xdev, axis=1)
    return (jnp.log10(degree), degree_freq, fit_slope, mean_log)


def solution(mesh):
    finer = Mesh(mesh.devices.reshape(4, 2, 2, 2, 8), ("row_0", "row_1", "row_2", "col_0", "col_1"))
    in_specs = (P(ROW_COL, None), P())
    out_specs = (P(None, ROW_COL), P(), P(), P())
    return jax.shard_map(
        on_device, mesh=finer, in_specs=in_specs, out_specs=out_specs, check_vma=False
    )
```

profile of v0, /device:TPU:1, one launch (start us, length us, event | category | flops | bytes accessed | tf_op | source)
XLA Modules:
  0.0 293.7 jit_solution(6370898261693356666)
XLA Ops:
  7.2 10.2 %all-gather = bf16[256,1024]{1,0:T(8,128)(2,1)} all-gather(bf16[128,1024]{1,0:T(8,128)(2,1)} %param.4), channel_id=2, replica_groups=mesh['row_0'=4,'row_1'=2,'row_2'=2,'col_0'=2,'col_1'=8] {'col_0'}, dimensions={0}, use_global_device_ids=true | all-gather | bytes 786432 | tf_op jit(solution)/shard_map/all_gather | solution.py:24
  20.0 7.0 %all-to-all-start = ((bf16[8,128,1024]{2,1,0:T(8,128)(2,1)}), bf16[8,128,1024]{2,1,0:T(8,128)(2,1)S(1)}, u32[]{:S(2)}, u32[]{:S(2)}) async-start(bf16[8,128,1024]{2,1,0:T(8,128)(2,1)} %broadcast_in_dim.22), calls=%async_computation | async-start | bytes 4194304 | tf_op jit(solution)/shard_map/all_to_all | solution.py:37
  27.1 29.8 %all-to-all-done = bf16[8,128,1024]{2,1,0:T(8,128)(2,1)S(1)} async-done(((bf16[8,128,1024]{2,1,0:T(8,128)(2,1)}), bf16[8,128,1024]{2,1,0:T(8,128)(2,1)S(1)}, u32[]{:S(2)}, u32[]{:S(2)}) %all-to-all-start) | async-done | bytes 2097184 | tf_op jit(solution)/shard_map/all_to_all | solution.py:37
  57.4 8.6 %all_to_all.15 = bf16[2,8,128,1024]{3,2,1,0:T(8,128)(2,1)S(1)} all-to-all(bf16[2,8,128,1024]{3,2,1,0:T(8,128)(2,1)S(1)} %broadcast_in_dim.23), channel_id=1, replica_groups=mesh['row_0'=4,'row_1'=2,'row_2'=2,'col_0'=2,'col_1'=8] {'row_2'}, dimensions={0} | all-to-all | bytes 8388608 | tf_op jit(solution)/shard_map/all_to_all | solution.py:37
  70.4 5.6 %all-gather.3.cloned.1.call-done = bf16[16,128,1024]{2,1,0:T(8,128)(2,1)} async-done(((bf16[2,128,1024]{2,1,0:T(8,128)(2,1)}), bf16[16,128,1024]{2,1,0:T(8,128)(2,1)}) %all-gather.3.cloned.1.call-update) | async-done | bytes 4194320 | tf_op jit(solution)/shard_map/all_gather | solution.py:24
  83.3 114.5 %while.13 = (s32[]{:T(128)}, f32[10,2048]{1,0:T(8,128)S(1)}, f32[10]{0:T(128)S(1)}, bf16[2048,1024]{1,0:T(8,128)(2,1)}, bf16[2048,1024]{1,0:T(8,128)(2,1)}, /*in...) while((s32[]{:T(128)}, f32[10,2048]{1,0:T(8,128)S(1)}, ...), condition=%wide.region_15.0_spmd, body=%wide.region_4.0_spmd.sunk | while | flops 1087373312 | bytes 4826379 | solution.py:109
  84.2 13.4 %exponential_reduce_fusion.11 = (f32[256]{0:T(256)S(1)}, f32[256]{0:T(256)S(1)}, f32[256]{0:T(256)S(1)}, f32[256]{0:T(256)S(1)}, f32[256]{0:T(256)S(1)}, /*index...) fusion(f32[]{:T(128)} %bitcast.64, f32[]{:T(128)} %bitcast.65, ...), kind=kOutput, calls=%fused_computation.6.clone.1 | convolution fusion | flops 1087370752 | bytes 4752388 | tf_op jit(solution)/shard_map/while/body/eval_jaxpr/dot_general | solution.py:93
  98.5 13.4 %exponential_reduce_fusion.11 = (f32[256]{0:T(256)S(1)}, f32[256]{0:T(256)S(1)}, f32[256]{0:T(256)S(1)}, f32[256]{0:T(256)S(1)}, f32[256]{0:T(256)S(1)}, /*index...) fusion(f32[]{:T(128)} %bitcast.64, f32[]{:T(128)} %bitcast.65, ...), kind=kOutput, calls=%fused_computation.6.clone.1 | convolution fusion | flops 1087370752 | bytes 4752388 | tf_op jit(solution)/shard_map/while/body/eval_jaxpr/dot_general | solution.py:93
  112.8 13.4 %exponential_reduce_fusion.11 = (f32[256]{0:T(256)S(1)}, f32[256]{0:T(256)S(1)}, f32[256]{0:T(256)S(1)}, f32[256]{0:T(256)S(1)}, f32[256]{0:T(256)S(1)}, /*index...) fusion(f32[]{:T(128)} %bitcast.64, f32[]{:T(128)} %bitcast.65, ...), kind=kOutput, calls=%fused_computation.6.clone.1 | convolution fusion | flops 1087370752 | bytes 4752388 | tf_op jit(solution)/shard_map/while/body/eval_jaxpr/dot_general | solution.py:93
  127.1 13.4 %exponential_reduce_fusion.11 = (f32[256]{0:T(256)S(1)}, f32[256]{0:T(256)S(1)}, f32[256]{0:T(256)S(1)}, f32[256]{0:T(256)S(1)}, f32[256]{0:T(256)S(1)}, /*index...) fusion(f32[]{:T(128)} %bitcast.64, f32[]{:T(128)} %bitcast.65, ...), kind=kOutput, calls=%fused_computation.6.clone.1 | convolution fusion | flops 1087370752 | bytes 4752388 | tf_op jit(solution)/shard_map/while/body/eval_jaxpr/dot_general | solution.py:93
  141.4 13.4 %exponential_reduce_fusion.11 = (f32[256]{0:T(256)S(1)}, f32[256]{0:T(256)S(1)}, f32[256]{0:T(256)S(1)}, f32[256]{0:T(256)S(1)}, f32[256]{0:T(256)S(1)}, /*index...) fusion(f32[]{:T(128)} %bitcast.64, f32[]{:T(128)} %bitcast.65, ...), kind=kOutput, calls=%fused_computation.6.clone.1 | convolution fusion | flops 1087370752 | bytes 4752388 | tf_op jit(solution)/shard_map/while/body/eval_jaxpr/dot_general | solution.py:93
  155.7 13.4 %exponential_reduce_fusion.11 = (f32[256]{0:T(256)S(1)}, f32[256]{0:T(256)S(1)}, f32[256]{0:T(256)S(1)}, f32[256]{0:T(256)S(1)}, f32[256]{0:T(256)S(1)}, /*index...) fusion(f32[]{:T(128)} %bitcast.64, f32[]{:T(128)} %bitcast.65, ...), kind=kOutput, calls=%fused_computation.6.clone.1 | convolution fusion | flops 1087370752 | bytes 4752388 | tf_op jit(solution)/shard_map/while/body/eval_jaxpr/dot_general | solution.py:93
  170.0 13.4 %exponential_reduce_fusion.11 = (f32[256]{0:T(256)S(1)}, f32[256]{0:T(256)S(1)}, f32[256]{0:T(256)S(1)}, f32[256]{0:T(256)S(1)}, f32[256]{0:T(256)S(1)}, /*index...) fusion(f32[]{:T(128)} %bitcast.64, f32[]{:T(128)} %bitcast.65, ...), kind=kOutput, calls=%fused_computation.6.clone.1 | convolution fusion | flops 1087370752 | bytes 4752388 | tf_op jit(solution)/shard_map/while/body/eval_jaxpr/dot_general | solution.py:93
  184.3 13.4 %exponential_reduce_fusion.11 = (f32[256]{0:T(256)S(1)}, f32[256]{0:T(256)S(1)}, f32[256]{0:T(256)S(1)}, f32[256]{0:T(256)S(1)}, f32[256]{0:T(256)S(1)}, /*index...) fusion(f32[]{:T(128)} %bitcast.64, f32[]{:T(128)} %bitcast.65, ...), kind=kOutput, calls=%fused_computation.6.clone.1 | convolution fusion | flops 1087370752 | bytes 4752388 | tf_op jit(solution)/shard_map/while/body/eval_jaxpr/dot_general | solution.py:93
  197.9 12.4 %all_to_all.16 = f32[16,10,128]{2,1,0:T(8,128)S(1)} all-to-all(f32[16,10,128]{2,1,0:T(8,128)S(1)} %copy.26), channel_id=1, replica_groups=mesh['row_0'=4,'row_1'=2,'row_2'=2,'col_0'=2,'col_1'=8] {'col_0','col_1'}, dimensions={0} | all-to-all | bytes 163840 | tf_op jit(solution)/shard_map/all_to_all | solution.py:55
  210.5 8.4 %pmax.35 = f32[10]{0:T(128)S(1)} all-reduce(f32[10]{0:T(128)S(1)} %reduce_max.9), channel_id=1, replica_groups=mesh['row_0'=4,'row_1'=2,'row_2'=2,'col_0'=2,'col_1'=8] {'row_0'}, use_global_device_ids=true, to_apply=%region_18.0 | all-reduce | flops 10 | bytes 80 | tf_op jit(solution)/shard_map/pmax | solution.py:60
  218.9 5.3 %pmax.36 = f32[10]{0:T(128)S(1)} all-reduce(f32[10]{0:T(128)S(1)} %pmax.35), channel_id=1, replica_groups=mesh['row_0'=4,'row_1'=2,'row_2'=2,'col_0'=2,'col_1'=8] {'row_1'}, use_global_device_ids=true, to_apply=%region_19.0 | all-reduce | flops 10 | bytes 80 | tf_op jit(solution)/shard_map/pmax | solution.py:60
  224.1 7.5 %pmax.37 = f32[10]{0:T(128)S(1)} all-reduce(f32[10]{0:T(128)S(1)} %pmax.36), channel_id=1, replica_groups=mesh['row_0'=4,'row_1'=2,'row_2'=2,'col_0'=2,'col_1'=8] {'row_2'}, use_global_device_ids=true, to_apply=%region_20.0 | all-reduce | flops 10 | bytes 80 | tf_op jit(solution)/shard_map/pmax | solution.py:60
  235.4 12.0 %pmax.39 = f32[10]{0:T(128)S(1)} all-reduce(f32[10]{0:T(128)S(1)} %pmax.38), channel_id=1, replica_groups=mesh['row_0'=4,'row_1'=2,'row_2'=2,'col_0'=2,'col_1'=8] {'col_1'}, use_global_device_ids=true, to_apply=%region_22.0 | all-reduce | flops 10 | bytes 80 | tf_op jit(solution)/shard_map/pmax | solution.py:60
  248.1 6.2 %all-reduce.1 = (f32[10,10]{1,0:T(8,128)S(1)}, f32[10]{0:T(128)S(1)}) all-reduce(f32[10,10]{1,0:T(8,128)S(1)} %maximum_reduce_fusion, f32[10]{0:T(128)S(1)} %get-tuple-element.169), channel_id=1, replica_groups=mesh['row_0'=4,'row_1'=2,'row_2'=2,'col_0'=2,'col_1'=8] {'row_0'}, use_global_device_ids=true, to_apply=%region_24.25 | all-reduce | flops 110 | bytes 880 | tf_op jit(solution)/shard_map/psum | solution.py:64
  254.3 5.4 %all-reduce.4 = (f32[10,10]{1,0:T(8,128)S(1)}, f32[10]{0:T(128)S(1)}) all-reduce(f32[10,10]{1,0:T(8,128)S(1)} %get-tuple-element.193, f32[10]{0:T(128)S(1)} %get-tuple-element.194), channel_id=1, replica_groups=mesh['row_0'=4,'row_1'=2,'row_2'=2,'col_0'=2,'col_1'=8] {'row_1'}, use_global_device_ids=true, to_apply=%region_25.26 | all-reduce | flops 110 | bytes 880 | tf_op jit(solution)/shard_map/psum | solution.py:64
  259.7 10.3 %all-reduce.3 = (f32[10,10]{1,0:T(8,128)S(1)}, f32[10]{0:T(128)S(1)}) all-reduce(f32[10,10]{1,0:T(8,128)S(1)} %get-tuple-element.199, f32[10]{0:T(128)S(1)} %get-tuple-element.200), channel_id=1, replica_groups=mesh['row_0'=4,'row_1'=2,'row_2'=2,'col_0'=2,'col_1'=8] {'row_2'}, use_global_device_ids=true, to_apply=%region_26.27 | all-reduce | flops 110 | bytes 880 | tf_op jit(solution)/shard_map/psum | solution.py:64
  270.0 3.9 %all-reduce.2 = (f32[10,10]{1,0:T(8,128)S(1)}, f32[10]{0:T(128)S(1)}) all-reduce(f32[10,10]{1,0:T(8,128)S(1)} %get-tuple-element.197, f32[10]{0:T(128)S(1)} %get-tuple-element.198), channel_id=1, replica_groups=mesh['row_0'=4,'row_1'=2,'row_2'=2,'col_0'=2,'col_1'=8] {'col_0'}, use_global_device_ids=true, to_apply=%region_27.28 | all-reduce | flops 110 | bytes 880 | tf_op jit(solution)/shard_map/psum | solution.py:64
  273.9 11.3 %all-reduce = (f32[10,10]{1,0:T(8,128)S(1)}, f32[10]{0:T(128)S(1)}) all-reduce(f32[10,10]{1,0:T(8,128)S(1)} %get-tuple-element.195, f32[10]{0:T(128)S(1)} %get-tuple-element.196), channel_id=1, replica_groups=mesh['row_0'=4,'row_1'=2,'row_2'=2,'col_0'=2,'col_1'=8] {'col_1'}, use_global_device_ids=true, to_apply=%region_28.29 | all-reduce | flops 110 | bytes 880 | tf_op jit(solution)/shard_map/psum | solution.py:64
  (79 shorter events, 28.3 us)
Async XLA Ops:
  7.2 68.8 %all-gather.3.cloned.1.call-start = ((), (), s32[]{:S(2)}) async-start(), calls=%async_computation.3 | async-start | bytes 4718592 | tf_op jit(solution)/shard_map/all_gather | solution.py:24
  20.0 7.0 %copy-start.2 = (s32[10]{0:T(128)S(1)}, s32[10]{0:T(128)}, u32[]{:S(2)}) copy-start(s32[10]{0:T(128)} %param.5) | copy-start | bytes 124
  20.0 36.8 %all-to-all-start = ((bf16[8,128,1024]{2,1,0:T(8,128)(2,1)}), bf16[8,128,1024]{2,1,0:T(8,128)(2,1)S(1)}, u32[]{:S(2)}, u32[]{:S(2)}) async-start(bf16[8,128,1024]{2,1,0:T(8,128)(2,1)} %broadcast_in_dim.22), calls=%async_computation | async-start | bytes 4194304 | tf_op jit(solution)/shard_map/all_to_all | solution.py:37
  76.0 3.4 %copy-start = (bf16[16,128,1024]{2,1,0:T(8,128)(2,1)S(1)}, bf16[16,128,1024]{2,1,0:T(8,128)(2,1)}, u32[]{:S(2)}) copy-start(bf16[16,128,1024]{2,1,0:T(8,128)(2,1)} %all-gather.3.cloned.1.call-done) | copy-start | bytes 12582916
  285.4 1.5 copy-start.1
Sparse Core Ops, SparseCore 0:
  17.6 58.3 all-gather.2
where the time goes:
time: 299 us; the launch traced here: 294 us
  matrix products  107 us (36%)
  blocking collectives  105 us (35%)
  waiting for transfers between devices  35.4 us (12%)
  local copies, waits for them, and re-layouts  15.5 us (5%)
  between operations  14.2 us (5%)
  other arithmetic  9.03 us (3%)
  starting transfers between devices  7.04 us (2%)
    dot_general x8, matrix products, one_block(): lax.dot_general(row_block, right_genes, (((1,), (1,)), ((), ())), preferr...  107 us
    psum x5, blocking collectives, over_axes_2(): return functools.reduce(lax.psum, axes, shard)  37.2 us
    pmax x5, blocking collectives, over_axes(): return functools.reduce(lax.pmax, axes, shard)  36.8 us
    all_to_all x1, waiting for transfers between devices, copy_for_each(): lax.all_to_all(jnp.broadcast_to(shard[None], (size, *shard.shape)), axis,...  29.8 us
    all_to_all x1, blocking collectives, summed_on_arrival(): lax.all_to_all(blocks, axis, split_axis=0, concat_axis=0, tiled=True)  12.4 us
    all_gather x1, blocking collectives, stacked_from(): blocks = lax.all_gather(blocks, axes[k], axis=0, tiled=True)  10.2 us
    all_to_all x1, blocking collectives, copy_for_each(): lax.all_to_all(jnp.broadcast_to(shard[None], (size, *shard.shape)), axis,...  8.58 us
    all_to_all x1, starting transfers between devices, copy_for_each(): lax.all_to_all(jnp.broadcast_to(shard[None], (size, *shard.shape)), axis,...  7 us
  transfers between devices with their start and end apart: 2, of which 2 were waited for; matrix products, arithmetic and copies ran while one was open for 3% of the time, Pallas kernels for 0%

commit v1 on v0

v1 whole, which is shorter than its diff:
```python
import functools
import math

import jax
import jax.numpy as jnp
from jax import lax
from jax.experimental import pallas as pl
from jax.experimental.pallas import tpu as pltpu
from jax.sharding import Mesh
from jax.sharding import PartitionSpec as P

F32 = jnp.float32
AXES = ("x", "yh", "core", "yl", "z")
NP = 10
BINS = 10
GENES = 32768
S = 1024
G = 128
MESH_ID = pl.DeviceIdType.MESH
OFFSETS = (
    0, 16, 1, 4, 112, 3, 116, 2, 124, 7, 32, 120, 96, 33, 35, 108, 11, 104, 34,
)
HOPS = (
    (0, 0, 0, 2), (0, 1, 1, 5), (0, 1, 4, 1), (0, 0, 5, 4), (0, 1, 2, 3), (0, 1, 5, 4), (0, 1, 0, 2), (0, 0,
    2, 3), (0, 0, 1, 5), (0, 0, 4, 1), (4, 0, 3, 8), (4, 0, 2, 6), (5, 1, 1, 7), (3, 1, 5, 6), (1, 1, 4, 10),
    (2, 0, 0, 7), (4, 1, 3, 8), (4, 1, 5, 12), (1, 0, 4, 10), (3, 0, 1, 9), (5, 1, 2, 9), (10, 1, 0, 13), (8,
    0, 3, 11), (10, 1, 1, 14), (4, 0, 5, 12), (6, 1, 2, 11), (10, 0, 0, 13), (12, 1, 3, 15), (9, 0, 2, 16),
    (10, 0, 1, 14), (8, 0, 5, 15), (13, 1, 0, 18), (9, 1, 2, 16), (11, 0, 5, 17), (15, 1, 3, 17), (13, 0, 0,
    18),
)
ARRIVALS = (
    (1, 1), (2, 0), (3, 1), (4, 0), (5, 1), (1, 0), (2, 1), (3, 0), (4, 1), (5, 0), (8, 0), (6, 0), (6, 1),
    (7, 0), (7, 1), (10, 1), (8, 1), (9, 0), (9, 1), (10, 0), (12, 1), (11, 0), (13, 1), (11, 1), (12, 0),
    (14, 1), (13, 0), (15, 1), (14, 0), (15, 0), (16, 0), (18, 1), (16, 1), (17, 0), (17, 1), (18, 0),
)
STEPS = ((1, 0, 0), (-1, 0, 0), (0, 1, 0), (0, -1, 0), (0, 0, 1), (0, 0, -1))
NS = len(OFFSETS)
PIECES = 2
ROWS = G // PIECES


def offset_of(e):
    return (e & 3, (e >> 2) & 3, e >> 4)


def minus(a, b):
    (ax, ay, az), (bx, by, bz) = offset_of(a), offset_of(b)
    return ((ax - bx) & 3) | (((ay - by) & 3) << 2) | (((az - bz) & 7) << 4)


def pair_plan():
    where = {e: i for i, e in enumerate(OFFSETS)}
    full, half = ({}, [])
    for d in range(1, 128):
        if minus(0, d) < d:
            continue
        found = []
        for i, e in enumerate(OFFSETS):
            j = where.get(minus(e, d))
            if j is not None:
                found.append((max(i, j), min(i, j)))
        later, earlier = min(found)
        if minus(0, d) == d:
            half.append((later, earlier, d))
        else:
            full.setdefault(later, []).append(earlier)
    return ({k: sorted(v) for k, v in full.items()}, half)


FULL, HALF = pair_plan()
LEFTS = sorted({0} | {a for v in FULL.values() for a in v} | {a for _, a, _ in HALF})
YROWS = max(max(v) - min(v) + 1 for v in [*FULL.values(), [0]])


def dot_t(a, b):
    return lax.dot_general(a, b, (((1,), (1,)), ((), ())), preferred_element_type=F32)


def coded(values, width):
    code = 0
    for v in reversed(values):
        code = code * width + v
    return code


def over_list(values, body):
    for k in range(0, len(values), 6):
        some = values[k : k + 6]

        def step(_, code):
            body(lax.rem(code, 32))
            return lax.div(code, 32)

        lax.fori_loop(0, len(some), step, jnp.int32(coded(some, 32)))


def powers_of(y, lefts, rights, exponents, rows_acc, cols_acc, halves):
    left_sum, left_inv = lefts
    mean = [jnp.broadcast_to(r[2:3, :], (8, 128)) for r in rights]
    inv = [jnp.broadcast_to(r[3:4, :], (8, 128)) for r in rights]
    cols = [[None] * halves for _ in range(NP)]
    for band in range(G // 8):
        rows = slice(8 * band, 8 * band + 8)
        m, i = (left_sum[rows, :], left_inv[rows, :])
        logs = [jnp.log2(jnp.abs((y(rows, h) - m * mean[h]) * i * inv[h])) for h in range(halves)]
        for p in range(NP):
            total = None
            for h in range(halves):
                q = jnp.exp2(exponents[p] * logs[h])
                cols[p][h] = q if cols[p][h] is None else cols[p][h] + q
                total = q if total is None else total + q
            rows_acc[p, rows, :] = rows_acc[p, rows, :] + total
    for p in range(NP):
        for h in range(halves):
            cols_acc(h, p, cols[p][h])


def lane_row(column):
    return jnp.broadcast_to(column, (128, 128)).T[0:8, :]


def kernel(
    pw, e, logdeg_out, freq_out, small_out,
    X, Y, YI, racc, cacc, LM, LI, ST, PS, RB, DG, ZA, ZB, tile, dsrc, fsrc,
    piece_send, piece_recv, pair_send, pair_recv, stat_send, stat_recv,
    part_send, part_recv, plane_send, plane_recv, za_send, za_recv, zb_send, zb_recv,
):
    px, pyh, c, pyl, pz = [lax.axis_index(a) for a in AXES]
    py = pyh * 2 + pyl
    other = 1 - c

    def at(dx, dy, dz, core):
        y = lax.rem(py + dy + 8, 4)
        return (lax.rem(px + dx + 8, 4), lax.div(y, 2), core, lax.rem(y, 2), lax.rem(pz + dz + 16, 8))

    def remote(src, dst, send, recv, device):
        return pltpu.make_async_remote_copy(
            src_ref=src, dst_ref=dst, send_sem=send, recv_sem=recv, device_id=device, device_id_type=MESH_ID
        )

    partner = at(0, 0, 0, other)
    exponents = [pw[p].astype(F32) for p in range(NP)]

    def piece(slot, q, half):
        return X.at[half, slot, ROWS * q : ROWS * q + ROWS, :]

    def own(q):
        return e.at[ROWS * q : ROWS * q + ROWS, :]

    def hop(i, q, k, j):
        dx, dy, dz = STEPS[k]
        src = own(q) if i == 0 else piece(i, q, c)
        return remote(src, piece(j, q, c), piece_send, piece_recv.at[j * PIECES + q], at(-dx, -dy, -dz, c))

    def to_partner(slot, q):
        src = own(q) if slot == 0 else piece(slot, q, c)
        return remote(src, piece(slot, q, c), pair_send, pair_recv.at[slot * PIECES + q], partner)

    for i, q, k, j in HOPS:
        if i == 0:
            hop(i, q, k, j).start()
    for q in range(PIECES):
        to_partner(0, q).start()

    X[c, 0, :, :] = e[...]
    values = e[...].astype(F32)
    total = jnp.sum(values, axis=1, keepdims=True)
    gene_mean = total * (1.0 / S)
    centred = values - gene_mean
    gene_inv = lax.rsqrt(jnp.sum(centred * centred, axis=1, keepdims=True) * (1.0 / S) + 1e-06)
    row_id = lax.broadcasted_iota(jnp.int32, (8, 128), 0)
    sum_row, inv_row = (lane_row(total), lane_row(gene_inv))
    stats = jnp.where(row_id == 0, sum_row, jnp.where(row_id == 1, inv_row, jnp.where(row_id == 2, sum_row * (1.0 / S), inv_row * (1.0 / S))))
    tile[...] = stats
    ST[pl.ds(c, 1)] = stats[None]

    def stat(slot, half):
        x, y, z = offset_of(OFFSETS[slot])
        return remote(tile, ST.at[2 * slot + c], stat_send, stat_recv.at[2 * slot + c], at(-x, -y, -z, half))

    def stat_in(slot, half):
        x, y, z = offset_of(OFFSETS[slot])
        return remote(tile, ST.at[2 * slot + half], stat_send, stat_recv.at[2 * slot + half], at(-x, -y, -z, half))

    stat(0, other).start()
    for slot in range(1, NS):
        for half in range(2):
            stat(slot, half).start()

    zero = jnp.zeros((NP, 8, 128), F32)

    def clear_rows(s, _):
        for b in range(G // 8):
            racc[s, :, 8 * b : 8 * b + 8, :] = zero
        return 0

    def clear_cols(s, _):
        cacc[s, 0] = zero
        cacc[s, 1] = zero
        return 0

    lax.fori_loop(0, NS, clear_rows, 0)
    lax.fori_loop(0, NS + 1, clear_cols, 0)
    for h in range(2):
        PS[:, h, :, :] = jnp.zeros((NS, 16, 128), F32)

    def ready(slot):
        for q in range(PIECES):
            remote(piece(slot, q, other), piece(slot, q, other), pair_send, pair_recv.at[slot * PIECES + q], partner).wait_recv()
        if slot == 0:
            stat_in(0, other).wait_recv()
        else:
            for half in range(2):
                stat_in(slot, half).wait_recv()
        if slot in LEFTS:
            mine = ST[2 * slot + c]
            LM[slot] = jnp.broadcast_to(mine[0:1, :], (128, 128)).T
            LI[slot] = jnp.broadcast_to(mine[1:2, :], (128, 128)).T

    def block(a, y_row, b, cols_slot):
        y_at = pl.multiple_of(y_row * G, G)

        def y(rows, h):
            return Y[pl.ds(y_at + rows.start, 8), 128 * h : 128 * h + 128]

        def add(h, p, v):
            cacc[cols_slot, h, p] = cacc[cols_slot, h, p] + v

        powers_of(y, (LM.at[a], LI.at[a]), [ST[2 * b], ST[2 * b + 1]], exponents, racc.at[a], add, 2)

    def rhs_of(b):
        return X[:, b].reshape(2 * G, S)

    ready(0)
    Y[0:G, :] = dot_t(X[c, 0], rhs_of(0))
    lax.fori_loop(0, 1, lambda _, x: (block(0, 0, 0, NS), x)[1], 0)

    seen = {s: 0 for s in range(1, NS)}
    for slot, q in ARRIVALS:
        remote(piece(slot, q, c), piece(slot, q, c), piece_send, piece_recv.at[slot * PIECES + q], partner).wait_recv()
        for h in HOPS:
            if h[0] == slot and h[1] == q:
                hop(*h).start()
        to_partner(slot, q).start()
        seen[slot] += 1
        if seen[slot] < PIECES:
            continue
        ready(slot)
        lefts = FULL.get(slot, [])
        if lefts:
            lo, hi = (min(lefts), max(lefts) + 1)
            Y[0 : (hi - lo) * G, :] = dot_t(X[c, lo:hi].reshape((hi - lo) * G, S), rhs_of(slot))
            over_list(lefts, lambda a, lo=lo, slot=slot: block(a, a - lo, slot, slot))
        for n, (b, a, _) in enumerate(HALF):
            if b == slot:
                YI[n] = dot_t(X[c, a], rhs_of(b))

    def half_block(n, d, a, b):
        x, y, z = offset_of(d)
        turn = lax.rem(lax.div(px, 2), 2) if x else lax.rem(lax.div(py, 2), 2) if y else lax.rem(lax.div(pz, 4), 2)
        h = lax.rem(c + turn, 2)

        def add(_, p, v):
            cacc[b, h, p] = cacc[b, h, p] + v

        lanes = pl.ds(pl.multiple_of(h * 128, 128), 128)
        powers_of(lambda rows, _: YI[n, rows, lanes], (LM.at[a], LI.at[a]), [ST[2 * b + h]], exponents, racc.at[a], add, 1)

    for n, (b, a, d) in enumerate(HALF):
        half_block(n, d, a, b)

    lane_id = lax.broadcasted_iota(jnp.int32, (128, 128), 1)

    def gather_cols(s, _):
        for h in range(2):
            PS[s, h, 0:NP, :] = jnp.sum(cacc[s, h], axis=1)
        return 0

    def gather_rows(s):
        sums = jnp.zeros((128, 128), F32)
        for p in range(NP):
            sums = jnp.where(lane_id == p, jnp.sum(racc[s, p], axis=1, keepdims=True), sums)
        PS[s, c, 0:NP, :] = PS[s, c, 0:NP, :] + sums.T[0:NP, :]

    lax.fori_loop(1, NS, gather_cols, 0)
    over_list(LEFTS, gather_rows)

    def part(slot, half):
        x, y, z = offset_of(OFFSETS[slot])
        return remote(PS.at[slot, half], RB.at[2 * slot + c], part_send, part_recv.at[2 * slot + c], at(x, y, z, half))

    for slot in range(1, NS):
        for half in range(2):
            part(slot, half).start()
    degree = PS[0, c]
    for slot in range(1, NS):
        for half in range(2):
            remote(PS.at[slot, half], RB.at[2 * slot + half], part_send, part_recv.at[2 * slot + half], partner).wait_recv()
    degree = lax.fori_loop(2, 2 * NS, lambda k, d: d + RB[k], degree)
    dsrc[...] = degree

    me = (px * 4 + py) * 2 + c
    DG[pl.ds(me, 1)] = degree[None]
    plane = [(dx, dy, dc) for dx in range(4) for dy in range(4) for dc in range(2) if (dx, dy, dc) != (0, 0, 0)]

    def plane_hop(n, dx, dy, dc):
        return remote(dsrc, DG.at[me], plane_send, plane_recv.at[n], at(dx, dy, 0, lax.rem(c + dc, 2)))

    def plane_in(n, dx, dy, dc):
        x, yh, core, yl, _ = at(-dx, -dy, 0, lax.rem(c + dc, 2))
        k = (x * 4 + yh * 2 + yl) * 2 + core
        return remote(dsrc, DG.at[k], plane_send, plane_recv.at[n], partner)

    for n, h in enumerate(plane):
        plane_hop(n, *h).start()
    logdeg_out[...] = (jnp.log(degree) * (1.0 / math.log(10.0)))[0:NP, :]
    for n, h in enumerate(plane):
        plane_in(n, *h).wait_recv()

    def most(k, m):
        return jnp.maximum(m, DG[k])

    top = jnp.broadcast_to(jnp.max(lax.fori_loop(1, 32, most, DG[0]), axis=1, keepdims=True), (16, 128))

    def ring(src, buf, send, recv):
        buf[pl.ds(pz, 1)] = src[...][None]
        for dz in range(1, 8):
            remote(src, buf.at[pz], send, recv.at[dz], at(0, 0, dz, c)).start()
        for dz in range(1, 8):
            remote(src, buf.at[lax.rem(pz - dz + 8, 8)], send, recv.at[dz], partner).wait_recv()

    dsrc2 = fsrc.at[0]
    dsrc2[...] = top
    ring(dsrc2, ZA, za_send, za_recv)
    peak = functools.reduce(jnp.maximum, [ZA[k] for k in range(8)])

    def weights(k, sums):
        d = DG[k]
        position = jnp.clip(BINS * d / peak - 0.5, 0.0, BINS - 1.0)
        near = [jnp.maximum(0.0, 1.0 - jnp.abs(position - float(b))) for b in range(BINS)]
        return tuple(s + v for s, v in zip(sums, [*near, d], strict=True))

    sums = lax.fori_loop(0, 32, weights, tuple(jnp.zeros((16, 128), F32) for _ in range(BINS + 1)))
    lanes = lax.broadcasted_iota(jnp.int32, (16, 128), 1)
    found = jnp.zeros((16, 128), F32)
    for b in range(BINS + 1):
        found = jnp.where(lanes == b, jnp.sum(sums[b], axis=1, keepdims=True), found)
    fsrc[1] = found
    ring(fsrc.at[1], ZB, zb_send, zb_recv)
    totals = functools.reduce(lambda u, v: u + v, [ZB[k] for k in range(8)])

    log10 = 1.0 / math.log(10.0)
    used = lanes < BINS
    freq = totals * (1.0 / GENES)
    fit_x = jnp.where(used, jnp.log((lanes.astype(F32) + 0.5) * peak / BINS) * log10, 0.0)
    fit_y = jnp.where(used, jnp.log(freq + 1.0 / GENES) * log10, 0.0)
    dev_x = jnp.where(used, fit_x - jnp.sum(fit_x, axis=1, keepdims=True) / BINS, 0.0)
    dev_y = jnp.where(used, fit_y - jnp.sum(fit_y, axis=1, keepdims=True) / BINS, 0.0)
    slope = jnp.sum(dev_x * dev_y, axis=1, keepdims=True) / jnp.sum(dev_x * dev_x, axis=1, keepdims=True)
    mean_log = jnp.log(freq[:, BINS : BINS + 1]) * log10
    freq_out[...] = freq[0:NP, 0:BINS]
    small_out[...] = jnp.where(lanes == 0, slope, mean_log)[0:NP, :]

    half_x = X.at[0]
    pltpu.make_async_copy(half_x.at[0 : NS - 1], half_x.at[0 : NS - 1], piece_send).wait()
    pltpu.make_async_copy(half_x, half_x, pair_send).wait()
    pltpu.make_async_copy(ST.at[0 : 2 * NS - 1], ST.at[0 : 2 * NS - 1], stat_send).wait()
    pltpu.make_async_copy(RB.at[0 : 2 * NS - 2], RB.at[0 : 2 * NS - 2], part_send).wait()
    pltpu.make_async_copy(DG.at[0:31], DG.at[0:31], plane_send).wait()
    pltpu.make_async_copy(ZA.at[0:7], ZA.at[0:7], za_send).wait()
    pltpu.make_async_copy(ZB.at[0:7], ZB.at[0:7], zb_send).wait()


def on_device(expression, powers):
    dma = pltpu.SemaphoreType.DMA
    vmem = pl.BlockSpec(memory_space=pltpu.VMEM)
    logdeg, freq, small = pl.pallas_call(
        kernel,
        out_shape=[
            jax.ShapeDtypeStruct((NP, G), F32),
            jax.ShapeDtypeStruct((NP, BINS), F32),
            jax.ShapeDtypeStruct((NP, 128), F32),
        ],
        in_specs=[pl.BlockSpec(memory_space=pltpu.SMEM), vmem],
        out_specs=[vmem] * 3,
        scratch_shapes=[
            pltpu.VMEM((2, NS, G, S), jnp.bfloat16),
            pltpu.VMEM((YROWS * G, 2 * G), F32),
            pltpu.VMEM((len(HALF), G, 2 * G), F32),
            pltpu.VMEM((NS, NP, G, 128), F32),
            pltpu.VMEM((NS + 1, 2, NP, 8, 128), F32),
            pltpu.VMEM((NS, G, 128), F32),
            pltpu.VMEM((NS, G, 128), F32),
            pltpu.VMEM((2 * NS, 8, 128), F32),
            pltpu.VMEM((NS, 2, 16, 128), F32),
            pltpu.VMEM((2 * NS, 16, 128), F32),
            pltpu.VMEM((32, 16, 128), F32),
            pltpu.VMEM((8, 16, 128), F32),
            pltpu.VMEM((8, 16, 128), F32),
            pltpu.VMEM((8, 128), F32),
            pltpu.VMEM((16, 128), F32),
            pltpu.VMEM((2, 16, 128), F32),
            dma, dma((NS * PIECES,)), dma, dma((NS * PIECES,)), dma, dma((2 * NS,)),
            dma, dma((2 * NS,)), dma, dma((31,)), dma, dma((8,)), dma, dma((8,)),
        ],
        compiler_params=pltpu.CompilerParams(has_side_effects=True, vmem_limit_bytes=60 * 2**20),
        name="scale_free_fit",
    )(powers, expression)
    return (logdeg, freq, small[:, 0], small[:, 1])


def solution(mesh):
    finer = Mesh(mesh.devices.reshape(4, 2, 2, 2, 8), AXES)
    return jax.shard_map(
        on_device,
        mesh=finer,
        in_specs=(P(AXES, None), P()),
        out_specs=(P(None, AXES), P(), P(), P()),
        check_vma=False,
    )
```

time: 299 us -> 120 us (0.40); the launches traced: 294 us -> 119 us
  Pallas kernels: 0 us -> 116 us
  matrix products: 107 us -> 0 us
  blocking collectives: 105 us -> 0 us
  waiting for transfers between devices: 35.4 us -> 0 us
  between operations: 14.2 us -> 0.65 us
  local copies, waits for them, and re-layouts: 15.5 us -> 2.78 us
  other arithmetic: 9.03 us -> 0 us
  starting transfers between devices: 7.04 us -> 0 us
    pallas_call x0 -> x1, Pallas kernels: none -> 116 us  [on_device(): pl.pallas_call(kernel, out_shape=[jax.ShapeDtypeStruct((NP, G), F32), jax...]
    dot_general x8 -> x0, matrix products: 107 us -> none  [one_block(): lax.dot_general(row_block, right_genes, (((1,), (1,)), ((), ())), preferr...]
    psum x5 -> x0, blocking collectives: 37.2 us -> none  [over_axes_2(): return functools.reduce(lax.psum, axes, shard)]
    pmax x5 -> x0, blocking collectives: 36.8 us -> none  [over_axes(): return functools.reduce(lax.pmax, axes, shard)]
    all_to_all x1 -> x0, waiting for transfers between devices: 29.8 us -> none  [copy_for_each(): lax.all_to_all(jnp.broadcast_to(shard[None], (size, *shard.shape)), axis,...]
    all_to_all x2 -> x0, blocking collectives: 21 us -> none  [the longest x1 12.4 us: summed_on_arrival(): lax.all_to_all(blocks, axis, split_axis=0, concat_axis=0, tiled=True)]
    all_gather x1 -> x0, blocking collectives: 10.2 us -> none  [stacked_from(): blocks = lax.all_gather(blocks, axes[k], axis=0, tiled=True)]
    reduce_sum x9 -> x0, other arithmetic: 7.14 us -> none  [the longest x2 3.59 us: gene_stats(): gene_mean = jnp.mean(values, axis=1)]
  transfers between devices with their start and end apart: 2 -> 0, of which waited for: 2 -> 0; matrix products, arithmetic and copies ran while one was open for 3% -> 0% of each run, Pallas kernels for 0% -> 0%
where the time goes in v1:
time: 120 us; the launch traced here: 119 us
  Pallas kernels  116 us (97%)
  local copies, waits for them, and re-layouts  2.78 us (2%)
    pallas_call x1, Pallas kernels, on_device(): pl.pallas_call(kernel, out_shape=[jax.ShapeDtypeStruct((NP, G), F32), jax...  116 us

profile of v1, /device:TPU:1, one launch (start us, length us, event | category | flops | bytes accessed | tf_op | source)
XLA Modules:
  0.0 119.0 jit_solution(6595179023006373365)
XLA Ops:
  0.6 115.6 %scale_free_fit.1 = (f32[10,128]{1,0:T(8,128)}, f32[10,10]{1,0:T(8,128)}, f32[10,128]{1,0:T(8,128)}) custom-call(s32[10]{0:T(128)} %pw.1, bf16[128,1024]{1,0:T(8,128)(2,1)} %e.1), custom_call_target="tpu_custom_call" | custom-call | tf_op jit(solution)/shard_map/scale_free_fit/pallas_call | solution.py:377
  116.2 0.0 copy-start.1
  116.3 1.5 %slice_reduce_fusion = (f32[10]{0:T(128)}, f32[10]{0:T(128)}) fusion(f32[10,128]{1,0:T(8,128)} %get-tuple-element.9), kind=kLoop, calls=%fused_computation | loop fusion | bytes 160 | tf_op jit(solution)/shard_map/slice | solution.py:409
  117.7 0.0 copy-done.1
  117.7 0.0 copy-start
  117.7 0.6 copy.8
  118.3 0.1 copy-done
  118.4 0.6 copy.9
Async XLA Ops:
  116.2 1.5 %copy-start.1 = (f32[10,128]{1,0:T(8,128)S(1)}, f32[10,128]{1,0:T(8,128)}, u32[]{:S(2)}) copy-start(f32[10,128]{1,0:T(8,128)} %get-tuple-element.16) | copy-start | bytes 15364
  117.7 0.7 copy-start

commit v2 on v1

v2 whole, which is shorter than its diff:
```python
import functools
import math

import jax
import jax.numpy as jnp
from jax import lax
from jax.experimental import pallas as pl
from jax.experimental.pallas import tpu as pltpu
from jax.sharding import Mesh
from jax.sharding import PartitionSpec as P

F32 = jnp.float32
AXES = ("x", "yh", "core", "yl", "z")
NP = 10
BINS = 10
GENES = 32768
S = 1024
G = 128
MESH_ID = pl.DeviceIdType.MESH
OFFSETS = (
    0, 16, 1, 4, 112, 3, 116, 2, 124, 7, 32, 120, 96, 33, 35, 108, 11, 104, 34,
)
HOPS = (
    (0, 0, 0, 2), (0, 1, 1, 5), (0, 1, 4, 1), (0, 0, 5, 4), (0, 1, 2, 3), (0, 1, 5, 4), (0, 1, 0, 2), (0, 0,
    2, 3), (0, 0, 1, 5), (0, 0, 4, 1), (4, 0, 3, 8), (4, 0, 2, 6), (5, 1, 1, 7), (3, 1, 5, 6), (1, 1, 4, 10),
    (2, 0, 0, 7), (4, 1, 3, 8), (4, 1, 5, 12), (1, 0, 4, 10), (3, 0, 1, 9), (5, 1, 2, 9), (10, 1, 0, 13), (8,
    0, 3, 11), (10, 1, 1, 14), (4, 0, 5, 12), (6, 1, 2, 11), (10, 0, 0, 13), (12, 1, 3, 15), (9, 0, 2, 16),
    (10, 0, 1, 14), (8, 0, 5, 15), (13, 1, 0, 18), (9, 1, 2, 16), (11, 0, 5, 17), (15, 1, 3, 17), (13, 0, 0,
    18),
)
ARRIVALS = (
    (1, 1), (2, 0), (3, 1), (4, 0), (5, 1), (1, 0), (2, 1), (3, 0), (4, 1), (5, 0), (8, 0), (6, 0), (6, 1),
    (7, 0), (7, 1), (10, 1), (8, 1), (9, 0), (9, 1), (10, 0), (12, 1), (11, 0), (13, 1), (11, 1), (12, 0),
    (14, 1), (13, 0), (15, 1), (14, 0), (15, 0), (16, 0), (18, 1), (16, 1), (17, 0), (17, 1), (18, 0),
)
PAIRS = (
    (2, 1, 1, 0, 4), (3, 0, 2, 0, 0), (4, 0, 1, 0, 0), (5, 0, 1, 0, 0), (5, 2, 3, 1, 0), (6, 0, 1, 0, 0), (6,
    2, 5, 0, 0), (7, 1, 6, 0, 0), (8, 0, 1, 0, 0), (8, 2, 3, 0, 0), (8, 5, 7, 0, 0), (9, 2, 8, 0, 0), (10, 2,
    4, 0, 0), (10, 5, 6, 0, 0), (10, 8, 9, 0, 0), (11, 2, 7, 0, 0), (12, 9, 10, 0, 3), (13, 4, 6, 0, 0), (13,
    8, 9, 0, 0), (13, 11, 12, 0, 0), (14, 4, 6, 0, 0), (14, 8, 11, 0, 0), (15, 2, 7, 0, 0), (15, 9, 10, 0, 0),
    (15, 13, 14, 0, 0), (16, 2, 7, 1, 0), (16, 13, 15, 0, 0), (17, 0, 1, 0, 0), (17, 2, 10, 0, 2), (17, 12,
    14, 2, 0), (18, 0, 4, 0, 0), (18, 6, 8, 0, 0), (18, 11, 12, 0, 1), (18, 15, 17, 0, 1),
)
STEPS = ((1, 0, 0), (-1, 0, 0), (0, 1, 0), (0, -1, 0), (0, 0, 1), (0, 0, -1))
NS = len(OFFSETS)
PIECES = 2
ROWS = G // PIECES


def offset_of(e):
    return (e & 3, (e >> 2) & 3, e >> 4)


def minus(a, b):
    (ax, ay, az), (bx, by, bz) = offset_of(a), offset_of(b)
    return ((ax - bx) & 3) | (((ay - by) & 3) << 2) | (((az - bz) & 7) << 4)


LEFTS = sorted({0} | {p[1] for p in PAIRS} | {p[2] for p in PAIRS})
LANES = 128


def coded(values, width):
    code = 0
    for v in reversed(values):
        code = code * width + v
    return code


def over_list(values, body):
    for k in range(0, len(values), 6):
        some = values[k : k + 6]

        def step(_, code):
            body(lax.rem(code, 32))
            return lax.div(code, 32)

        lax.fori_loop(0, len(some), step, jnp.int32(coded(some, 32)))


def powers_of(y, lefts, rights, keep, exponents, rows_acc, cols_acc):
    left_sum, left_inv = lefts
    mean = [jnp.broadcast_to(r[2:3, :], (8, 128)) for r in rights]
    inv = [jnp.broadcast_to(r[3:4, :], (8, 128)) * k for r, k in zip(rights, keep, strict=True)]
    cols = [[None] * 2 for _ in range(NP)]
    for band in range(G // 8):
        rows = slice(8 * band, 8 * band + 8)
        m, i = (left_sum[rows, :], left_inv[rows, :])
        logs = [jnp.log2(jnp.abs((y[rows, 128 * h : 128 * h + 128] - m * mean[h]) * i * inv[h])) for h in range(2)]
        for p in range(NP):
            qs = [jnp.exp2(exponents[p] * v) for v in logs]
            cols[p] = [q if old is None else old + q for old, q in zip(cols[p], qs, strict=True)]
            rows_acc[p, rows, :] = rows_acc[p, rows, :] + (qs[0] + qs[1])
    for p in range(NP):
        for h in range(2):
            cols_acc[h, p] = cols_acc[h, p] + cols[p][h]


def lane_row(column):
    return jnp.broadcast_to(column, (128, 128)).T[0:8, :]


def kernel(
    pw, e, logdeg_out, freq_out, small_out,
    X, Y, racc, cacc, LM, LI, ST, PS, RB, DG, ZA, PA, ZB, tile, dsrc, zsrc, fsrc,
    piece_send, piece_recv, pair_send, pair_recv, stat_send, stat_recv,
    part_send, part_recv, plane_send, plane_recv, za_send, za_recv, pa_send, pa_recv, zb_send, zb_recv, acc0, acc1,
):
    px, pyh, c, pyl, pz = [lax.axis_index(a) for a in AXES]
    py = pyh * 2 + pyl
    other = 1 - c

    def at(dx, dy, dz, core):
        y = lax.rem(py + dy + 8, 4)
        return (lax.rem(px + dx + 8, 4), lax.div(y, 2), core, lax.rem(y, 2), lax.rem(pz + dz + 16, 8))

    def remote(src, dst, send, recv, device):
        return pltpu.make_async_remote_copy(
            src_ref=src, dst_ref=dst, send_sem=send, recv_sem=recv, device_id=device, device_id_type=MESH_ID
        )

    partner = at(0, 0, 0, other)
    exponents = [pw[p].astype(F32) for p in range(NP)]

    def piece(slot, q, half):
        return X.at[half, slot, ROWS * q : ROWS * q + ROWS, :]

    def own(q):
        return e.at[ROWS * q : ROWS * q + ROWS, :]

    def hop(i, q, k, j):
        dx, dy, dz = STEPS[k]
        src = own(q) if i == 0 else piece(i, q, c)
        return remote(src, piece(j, q, c), piece_send, piece_recv.at[j * PIECES + q], at(-dx, -dy, -dz, c))

    def to_partner(slot, q):
        src = own(q) if slot == 0 else piece(slot, q, c)
        return remote(src, piece(slot, q, c), pair_send, pair_recv.at[slot * PIECES + q], partner)


    greeted = set()
    for e_ in OFFSETS:
        x, y, z = offset_of(e_)
        for dc in range(2):
            greeted |= {(x, y, z, dc), (-x % 4, -y % 4, -z % 8, dc)}
    for dx, dy, dz in STEPS:
        greeted.add((dx % 4, dy % 4, dz % 8, 0))
    for dc in range(2):
        greeted |= {(dx, dy, 0, dc) for dx in range(4) for dy in range(4)}
    greeted |= {(0, 0, dz, 0) for dz in range(8)}
    greeted = sorted(greeted - {(0, 0, 0, 0)}, key=lambda d: -sum(min(v, n - v) for v, n in zip(d, (4, 4, 8, 2), strict=True)))
    barrier = pltpu.get_barrier_semaphore()
    for dx, dy, dz, dc in greeted:
        pl.semaphore_signal(barrier, inc=1, device_id=at(dx, dy, dz, lax.rem(c + dc, 2)), device_id_type=MESH_ID)

    X[c, 0, :, :] = e[...]
    values = e[...].astype(F32)
    total = jnp.sum(values, axis=1, keepdims=True)
    gene_mean = total * (1.0 / S)
    centred = values - gene_mean
    gene_inv = lax.rsqrt(jnp.sum(centred * centred, axis=1, keepdims=True) * (1.0 / S) + 1e-06)
    row_id = lax.broadcasted_iota(jnp.int32, (8, 128), 0)
    sum_row, inv_row = (lane_row(total), lane_row(gene_inv))
    stats = jnp.where(row_id == 0, sum_row, jnp.where(row_id == 1, inv_row, jnp.where(row_id == 2, sum_row * (1.0 / S), inv_row * (1.0 / S))))
    tile[...] = stats
    ST[pl.ds(c, 1)] = stats[None]

    def stat(slot, half):
        x, y, z = offset_of(OFFSETS[slot])
        return remote(tile, ST.at[2 * slot + c], stat_send, stat_recv.at[2 * slot + c], at(-x, -y, -z, half))

    def stat_in(slot, half):
        x, y, z = offset_of(OFFSETS[slot])
        return remote(tile, ST.at[2 * slot + half], stat_send, stat_recv.at[2 * slot + half], at(-x, -y, -z, half))

    zero = jnp.zeros((NP, 8, 128), F32)

    def clear_rows(s, _):
        for b in range(G // 8):
            racc[s, :, 8 * b : 8 * b + 8, :] = zero
        return 0

    def clear_cols(s, _):
        cacc[s, 0] = zero
        cacc[s, 1] = zero
        return 0

    lax.fori_loop(0, NS, clear_rows, 0)
    lax.fori_loop(0, NS + 1, clear_cols, 0)
    for h in range(2):
        PS[:, h, :, :] = jnp.zeros((NS, 16, 128), F32)

    pl.semaphore_wait(barrier, len(greeted))
    for q in range(PIECES):
        to_partner(0, q).start()
    stat(0, other).start()
    for slot in range(1, NS):
        for half in range(2):
            stat(slot, half).start()
    for i, q, k, j in HOPS:
        if i == 0:
            hop(i, q, k, j).start()

    def ready(slot):
        for q in range(PIECES):
            remote(piece(slot, q, other), piece(slot, q, other), pair_send, pair_recv.at[slot * PIECES + q], partner).wait_recv()
        if slot == 0:
            stat_in(0, other).wait_recv()
        else:
            for half in range(2):
                stat_in(slot, half).wait_recv()
        if slot in LEFTS:
            mine = ST[2 * slot + c]
            LM[slot] = jnp.broadcast_to(mine[0:1, :], (128, 128)).T
            LI[slot] = jnp.broadcast_to(mine[1:2, :], (128, 128)).T

    turns = (lax.rem(lax.div(px, 2), 2), lax.rem(lax.div(py, 2), 2), lax.rem(lax.div(pz, 4), 2))

    def kept(mark):
        turn = jnp.where(mark == 1, turns[0], jnp.where(mark == 2, turns[1], turns[2]))
        h = lax.rem(c + turn, 2)
        return [jnp.where(mark == 0, 1.0, jnp.where(mark == 4, 0.0, jnp.where(h == k, 1.0, 0.0))) for k in range(2)]

    def multiply(b, a0, a1):
        for k in range(2):
            for u in range(2):
                cols = slice(256 * (2 * u + k), 256 * (2 * u + k) + 256)
                rhs = jnp.concatenate([X[0, b, :, cols], X[1, b, :, cols]], axis=0)
                pltpu.matmul_push_rhs(rhs, staging_register=k, mxu_index=u, transpose=True)
        for k in range(2):
            for u, acc in ((0, acc0), (1, acc1)):
                cols = slice(256 * (2 * u + k), 256 * (2 * u + k) + 256)
                lhs = jnp.concatenate([X[c, a0, :, cols], X[c, a1, :, cols]], axis=0)
                pltpu.matmul_acc_lhs(acc, lhs, load_staged_rhs=k)

    def take():
        z = pltpu.matmul_pop(acc0) + pltpu.matmul_pop(acc1)
        Y[0] = z[0:G]
        Y[1] = z[G : 2 * G]

    def use(n, a, b, cols_slot, mark):
        powers_of(Y.at[n], (LM.at[a], LI.at[a]), [ST[2 * b], ST[2 * b + 1]], kept(mark), exponents, racc.at[a], cacc.at[cols_slot])

    def run(pairs, after):
        for k in range(0, len(pairs), 5):
            some = pairs[k : k + 5]
            rest = pairs[k + 5 : k + 6] or [after]
            digits = [coded([p[n] for p in [*some, *rest]], 32) for n in range(3)]
            marks = coded([p[3] * 8 + p[4] for p in some], 64)

            def step(_, codes):
                rights, left0, left1, both = codes
                b, a0, a1, mark = (lax.rem(rights, 32), lax.rem(left0, 32), lax.rem(left1, 32), lax.rem(both, 64))
                rights, left0, left1 = (lax.div(rights, 32), lax.div(left0, 32), lax.div(left1, 32))
                take()
                multiply(lax.rem(rights, 32), lax.rem(left0, 32), lax.rem(left1, 32))
                use(0, a0, b, b, lax.div(mark, 8))
                use(1, a1, b, b, lax.rem(mark, 8))
                return (rights, left0, left1, lax.div(both, 64))

            lax.fori_loop(0, len(some), step, tuple(jnp.int32(v) for v in [*digits, marks]))

    pltpu.matmul_pop(acc0)
    pltpu.matmul_pop(acc1)

    ready(0)
    multiply(0, 0, 0)
    take()

    def own_block(_, x):
        use(0, 0, 0, NS, 0)
        return x

    lax.fori_loop(0, 1, own_block, 0)

    handled = {(0, 0), (0, 1)}
    waiting = list(ARRIVALS)

    def arrive(last):
        while any((last, q) not in handled for q in range(PIECES)):
            slot, q = waiting.pop(0)
            handled.add((slot, q))
            remote(piece(slot, q, c), piece(slot, q, c), piece_send, piece_recv.at[slot * PIECES + q], partner).wait_recv()
            for h in HOPS:
                if h[0] == slot and h[1] == q:
                    hop(*h).start()
            to_partner(slot, q).start()

    known = [0]

    def prepare(last):
        while known[0] < last:
            known[0] += 1
            ready(known[0])

    stages = sorted({p[0] for p in PAIRS})
    arrive(stages[0])
    arrive(stages[1])
    prepare(stages[0])
    first = next(p for p in PAIRS if p[0] == stages[0])
    multiply(*first[0:3])
    for n, b in enumerate(stages):
        arrive(stages[min(n + 2, len(stages) - 1)])
        prepare(stages[min(n + 1, len(stages) - 1)])
        here = [p for p in PAIRS if p[0] == b]
        after = next((p for p in PAIRS if p[0] > b), PAIRS[-1])
        run(here, after)
    pltpu.matmul_pop(acc0)
    pltpu.matmul_pop(acc1)

    def gather_cols(s, _):
        for h in range(2):
            PS[s, h, 0:NP, :] = jnp.sum(cacc[s, h], axis=1)
        return 0

    def gather_rows(s):
        for p in range(NP):
            sums = jnp.sum(racc[s, p].T.reshape(16, 8, 128), axis=0)
            PS[s, c, p : p + 1, :] = PS[s, c, p : p + 1, :] + jnp.sum(sums, axis=0, keepdims=True)

    def part(slot, half):
        x, y, z = offset_of(OFFSETS[slot])
        return remote(PS.at[slot, half], RB.at[2 * slot + c], part_send, part_recv.at[2 * slot + c], at(x, y, z, half))

    def send_parts(slots):
        for slot in slots:
            if slot > 0:
                for half in range(2):
                    part(slot, half).start()

    def far(slot):
        x, y, z = offset_of(OFFSETS[slot])
        return min(x, 4 - x) + min(y, 4 - y) + min(z, 8 - z)

    lax.fori_loop(1, NS, gather_cols, 0)
    send_parts([s for s in range(1, NS) if s not in LEFTS])
    by_distance = sorted(LEFTS, key=lambda s: -far(s))
    for k in range(0, len(by_distance), 6):
        over_list(by_distance[k : k + 6], gather_rows)
        send_parts(by_distance[k : k + 6])
    degree = PS[0, c]
    for slot in range(1, NS):
        for half in range(2):
            remote(PS.at[slot, half], RB.at[2 * slot + half], part_send, part_recv.at[2 * slot + half], partner).wait_recv()
    degree = lax.fori_loop(2, 2 * NS, lambda k, d: d + RB[k], degree)
    dsrc[...] = degree

    me = (px * 4 + py) * 2 + c
    DG[pl.ds(me, 1)] = degree[None]
    plane = [(dx, dy, dc) for dx in range(4) for dy in range(4) for dc in range(2) if (dx, dy, dc) != (0, 0, 0)]

    def plane_hop(n, dx, dy, dc):
        return remote(dsrc, DG.at[me], plane_send, plane_recv.at[n], at(dx, dy, 0, lax.rem(c + dc, 2)))

    def plane_id(dx, dy, dc):
        x, yh, core, yl, _ = at(-dx, -dy, 0, lax.rem(c + dc, 2))
        return (x * 4 + yh * 2 + yl) * 2 + core

    diagonal = lax.broadcasted_iota(jnp.int32, (16, 128), 0) == lax.broadcasted_iota(jnp.int32, (16, 128), 1)

    def to_row(column):
        return jnp.sum(jnp.where(diagonal, column, 0.0), axis=0, keepdims=True)

    def ring(src, buf, send, recv):
        for dz in range(1, 8):
            remote(src, buf.at[pz], send, recv.at[dz], at(0, 0, dz, c)).start()

    def ring_in(src, buf, send, recv):
        for dz in range(1, 8):
            remote(src, buf.at[lax.rem(pz - dz + 8, 8)], send, recv.at[dz], partner).wait_recv()

    mine = to_row(jnp.max(degree, axis=1, keepdims=True))
    zsrc[0] = mine
    ring(zsrc.at[0], ZA, za_send, za_recv)
    for n, h in enumerate(plane):
        plane_hop(n, *h).start()
    logdeg_out[...] = (jnp.log(degree) * (1.0 / math.log(10.0)))[0:NP, :]
    ZA[pl.ds(pz, 1)] = mine[None]
    ring_in(zsrc.at[0], ZA, za_send, za_recv)
    mine = functools.reduce(jnp.maximum, [ZA[k] for k in range(8)])
    zsrc[1] = mine
    for n, (dx, dy, dc) in enumerate(plane):
        remote(zsrc.at[1], PA.at[me], pa_send, pa_recv.at[n], at(dx, dy, 0, lax.rem(c + dc, 2))).start()
    PA[pl.ds(me, 1)] = mine[None]
    for n, h in enumerate(plane):
        remote(dsrc, DG.at[plane_id(*h)], plane_send, plane_recv.at[n], partner).wait_recv()
    for n, h in enumerate(plane):
        remote(zsrc.at[1], PA.at[plane_id(*h)], pa_send, pa_recv.at[n], partner).wait_recv()
    peak_row = functools.reduce(jnp.maximum, [PA[k] for k in range(32)])
    peak = jnp.broadcast_to(jnp.sum(jnp.where(diagonal, peak_row, 0.0), axis=1, keepdims=True), (16, 128))

    def weights(k, sums):
        d = DG[k]
        position = jnp.clip(BINS * d / peak - 0.5, 0.0, BINS - 1.0)
        near = [jnp.maximum(0.0, 1.0 - jnp.abs(position - float(b))) for b in range(BINS)]
        return tuple(s + v for s, v in zip(sums, [*near, d], strict=True))

    sums = lax.fori_loop(0, 32, weights, tuple(jnp.zeros((16, 128), F32) for _ in range(BINS + 1)))
    lanes = lax.broadcasted_iota(jnp.int32, (16, 128), 1)
    found = jnp.zeros((16, 128), F32)
    for b in range(BINS + 1):
        found = jnp.where(lanes == b, jnp.sum(sums[b], axis=1, keepdims=True), found)
    fsrc[...] = found
    ring(fsrc, ZB, zb_send, zb_recv)
    ZB[pl.ds(pz, 1)] = found[None]
    ring_in(fsrc, ZB, zb_send, zb_recv)
    totals = functools.reduce(lambda u, v: u + v, [ZB[k] for k in range(8)])

    log10 = 1.0 / math.log(10.0)
    used = lanes < BINS
    freq = totals * (1.0 / GENES)
    fit_x = jnp.where(used, jnp.log((lanes.astype(F32) + 0.5) * peak / BINS) * log10, 0.0)
    fit_y = jnp.where(used, jnp.log(freq + 1.0 / GENES) * log10, 0.0)
    dev_x = jnp.where(used, fit_x - jnp.sum(fit_x, axis=1, keepdims=True) / BINS, 0.0)
    dev_y = jnp.where(used, fit_y - jnp.sum(fit_y, axis=1, keepdims=True) / BINS, 0.0)
    slope = jnp.sum(dev_x * dev_y, axis=1, keepdims=True) / jnp.sum(dev_x * dev_x, axis=1, keepdims=True)
    mean_log = jnp.log(freq[:, BINS : BINS + 1]) * log10
    freq_out[...] = freq[0:NP, 0:BINS]
    small_out[0:1, :] = to_row(slope)
    small_out[1:2, :] = to_row(mean_log)

    half_x = X.at[0]
    pltpu.make_async_copy(half_x.at[0 : NS - 1], half_x.at[0 : NS - 1], piece_send).wait()
    pltpu.make_async_copy(half_x, half_x, pair_send).wait()
    pltpu.make_async_copy(ST.at[0 : 2 * NS - 1], ST.at[0 : 2 * NS - 1], stat_send).wait()
    pltpu.make_async_copy(RB.at[0 : 2 * NS - 2], RB.at[0 : 2 * NS - 2], part_send).wait()
    pltpu.make_async_copy(DG.at[0:31], DG.at[0:31], plane_send).wait()
    pltpu.make_async_copy(ZA.at[0:7], ZA.at[0:7], za_send).wait()
    pltpu.make_async_copy(PA.at[0:31], PA.at[0:31], pa_send).wait()
    pltpu.make_async_copy(ZB.at[0:7], ZB.at[0:7], zb_send).wait()


def on_device(expression, powers):
    dma = pltpu.SemaphoreType.DMA
    vmem = pl.BlockSpec(memory_space=pltpu.VMEM)
    def body(*refs):
        pl.run_scoped(functools.partial(kernel, *refs), pltpu.ACC(0)((2 * G, 256), F32), pltpu.ACC(1)((2 * G, 256), F32))

    logdeg, freq, small = pl.pallas_call(
        body,
        out_shape=[
            jax.ShapeDtypeStruct((NP, G), F32),
            jax.ShapeDtypeStruct((NP, BINS), F32),
            jax.ShapeDtypeStruct((2, 128), F32),
        ],
        in_specs=[pl.BlockSpec(memory_space=pltpu.SMEM), vmem],
        out_specs=[vmem] * 3,
        scratch_shapes=[
            pltpu.VMEM((2, NS, G, S), jnp.bfloat16),
            pltpu.VMEM((2, G, 2 * G), F32),
            pltpu.VMEM((NS, NP, G, 128), F32),
            pltpu.VMEM((NS + 1, 2, NP, 8, 128), F32),
            pltpu.VMEM((NS, G, 128), F32),
            pltpu.VMEM((NS, G, 128), F32),
            pltpu.VMEM((2 * NS, 8, 128), F32),
            pltpu.VMEM((NS, 2, 16, 128), F32),
            pltpu.VMEM((2 * NS, 16, 128), F32),
            pltpu.VMEM((32, 16, 128), F32),
            pltpu.VMEM((8, 1, 128), F32),
            pltpu.VMEM((32, 1, 128), F32),
            pltpu.VMEM((8, 16, 128), F32),
            pltpu.VMEM((8, 128), F32),
            pltpu.VMEM((16, 128), F32),
            pltpu.VMEM((2, 1, 128), F32),
            pltpu.VMEM((16, 128), F32),
            dma, dma((NS * PIECES,)), dma, dma((NS * PIECES,)), dma, dma((2 * NS,)),
            dma, dma((2 * NS,)), dma, dma((31,)), dma, dma((8,)), dma, dma((31,)), dma, dma((8,)),
        ],
        compiler_params=pltpu.CompilerParams(collective_id=0, has_side_effects=True, vmem_limit_bytes=60 * 2**20),
        name="scale_free_fit",
    )(powers, expression)
    return (logdeg, freq, small[0, 0:NP], small[1, 0:NP])


def solution(mesh):
    finer = Mesh(mesh.devices.reshape(4, 2, 2, 2, 8), AXES)
    return jax.shard_map(
        on_device,
        mesh=finer,
        in_specs=(P(AXES, None), P()),
        out_specs=(P(None, AXES), P(), P(), P()),
        check_vma=False,
    )
```

time: 120 us -> 79.4 us (0.66)
  Pallas kernels: 116 us -> 76.1 us
    pallas_call x1, Pallas kernels: 116 us -> 76.1 us  [on_device(): pl.pallas_call(body, out_shape=[jax.ShapeDtypeStruct((NP, G), F32), jax.S...]
    slice x1 -> x0, local copies, waits for them, and re-layouts: 1.47 us -> none  [on_device(): return (logdeg, freq, small[:, 0], small[:, 1])]
    squeeze x0 -> x1, local copies, waits for them, and re-layouts: none -> 1.22 us  [on_device(): return (logdeg, freq, small[0, 0:NP], small[1, 0:NP])]
where the time goes in v2:
time: 79.4 us; the launch traced here: 79.3 us
  Pallas kernels  76.1 us (96%)
  local copies, waits for them, and re-layouts  2.52 us (3%)
    pallas_call x1, Pallas kernels, on_device(): pl.pallas_call(body, out_shape=[jax.ShapeDtypeStruct((NP, G), F32), jax.S...  76.1 us

profile of v2, /device:TPU:1, one launch (start us, length us, event | category | flops | bytes accessed | tf_op | source)
XLA Modules:
  0.0 79.3 jit_solution(16748647294800902973)
XLA Ops:
  0.6 76.1 %scale_free_fit.1 = (f32[10,128]{1,0:T(8,128)}, f32[10,10]{1,0:T(8,128)}, f32[2,128]{1,0:T(2,128)}) custom-call(s32[10]{0:T(128)} %refs_0_.1, bf16[128,1024]{1,0:T(8,128)(2,1)} %refs_1_.1), custom_call_target="tpu_custom_call" | custom-call | tf_op jit(solution)/shard_map/scale_free_fit/pallas_call | solution.py:439
  76.7 0.0 copy-start.1
  76.7 1.2 %slice_bitcast_fusion = (f32[10]{0:T(128)}, f32[10]{0:T(128)}) fusion(f32[2,128]{1,0:T(2,128)} %get-tuple-element.9), kind=kLoop, calls=%fused_computation | loop fusion | bytes 160 | tf_op jit(solution)/shard_map/squeeze | solution.py:472
  78.0 0.0 copy-done.1
  78.0 0.0 copy-start
  78.0 0.6 copy.8
  78.6 0.1 copy-done
  78.7 0.6 copy.9
Async XLA Ops:
  76.7 1.2 %copy-start.1 = (f32[10,128]{1,0:T(8,128)S(1)}, f32[10,128]{1,0:T(8,128)}, u32[]{:S(2)}) copy-start(f32[10,128]{1,0:T(8,128)} %get-tuple-element.16) | copy-start | bytes 15364
  78.0 0.7 copy-start

commit v3 on v2

--- a/solution.py
+++ b/solution.py
@@ -56,6 +56,7 @@
     return ((ax - bx) & 3) | (((ay - by) & 3) << 2) | (((az - bz) & 7) << 4)
 
 
+FIRST = {j: q for i, q, k, j in reversed(HOPS)}
 LEFTS = sorted({0} | {p[1] for p in PAIRS} | {p[2] for p in PAIRS})
 LANES = 128
 
@@ -97,7 +98,7 @@
 
 
 def lane_row(column):
-    return jnp.broadcast_to(column, (128, 128)).T[0:8, :]
+    return jnp.broadcast_to(column, (128, 128)).T[0:4, :]
 
 
 def kernel(
@@ -159,7 +160,7 @@
     gene_mean = total * (1.0 / S)
     centred = values - gene_mean
     gene_inv = lax.rsqrt(jnp.sum(centred * centred, axis=1, keepdims=True) * (1.0 / S) + 1e-06)
-    row_id = lax.broadcasted_iota(jnp.int32, (8, 128), 0)
+    row_id = lax.broadcasted_iota(jnp.int32, (4, 128), 0)
     sum_row, inv_row = (lane_row(total), lane_row(gene_inv))
     stats = jnp.where(row_id == 0, sum_row, jnp.where(row_id == 1, inv_row, jnp.where(row_id == 2, sum_row * (1.0 / S), inv_row * (1.0 / S))))
     tile[...] = stats
@@ -193,22 +194,20 @@
     pl.semaphore_wait(barrier, len(greeted))
     for q in range(PIECES):
         to_partner(0, q).start()
+    for i, q, k, j in HOPS:
+        if i == 0 and q == FIRST[j]:
+            hop(i, q, k, j).start()
     stat(0, other).start()
     for slot in range(1, NS):
-        for half in range(2):
-            stat(slot, half).start()
+        stat(slot, c).start()
     for i, q, k, j in HOPS:
-        if i == 0:
+        if i == 0 and q != FIRST[j]:
             hop(i, q, k, j).start()
 
     def ready(slot):
         for q in range(PIECES):
             remote(piece(slot, q, other), piece(slot, q, other), pair_send, pair_recv.at[slot * PIECES + q], partner).wait_recv()
-        if slot == 0:
-            stat_in(0, other).wait_recv()
-        else:
-            for half in range(2):
-                stat_in(slot, half).wait_recv()
+        stat_in(slot, other).wait_recv()
         if slot in LEFTS:
             mine = ST[2 * slot + c]
             LM[slot] = jnp.broadcast_to(mine[0:1, :], (128, 128)).T
@@ -285,6 +284,9 @@
                 if h[0] == slot and h[1] == q:
                     hop(*h).start()
             to_partner(slot, q).start()
+            if all((slot, k) in handled for k in range(PIECES)):
+                stat_in(slot, c).wait_recv()
+                remote(ST.at[2 * slot + c], ST.at[2 * slot + c], stat_send, stat_recv.at[2 * slot + c], partner).start()
 
     known = [0]
 
@@ -320,7 +322,7 @@
 
     def part(slot, half):
         x, y, z = offset_of(OFFSETS[slot])
-        return remote(PS.at[slot, half], RB.at[2 * slot + c], part_send, part_recv.at[2 * slot + c], at(x, y, z, half))
+        return remote(PS.at[slot, half, 0:NP], RB.at[2 * slot + c], part_send, part_recv.at[2 * slot + c], at(x, y, z, half))
 
     def send_parts(slots):
         for slot in slots:
@@ -338,25 +340,25 @@
     for k in range(0, len(by_distance), 6):
         over_list(by_distance[k : k + 6], gather_rows)
         send_parts(by_distance[k : k + 6])
-    degree = PS[0, c]
+    degree = PS[0, c, 0:NP, :]
     for slot in range(1, NS):
         for half in range(2):
-            remote(PS.at[slot, half], RB.at[2 * slot + half], part_send, part_recv.at[2 * slot + half], partner).wait_recv()
+            remote(PS.at[slot, half, 0:NP], RB.at[2 * slot + half], part_send, part_recv.at[2 * slot + half], partner).wait_recv()
     degree = lax.fori_loop(2, 2 * NS, lambda k, d: d + RB[k], degree)
-    dsrc[...] = degree
+    dsrc[0:NP, :] = degree
 
     me = (px * 4 + py) * 2 + c
     DG[pl.ds(me, 1)] = degree[None]
     plane = [(dx, dy, dc) for dx in range(4) for dy in range(4) for dc in range(2) if (dx, dy, dc) != (0, 0, 0)]
 
     def plane_hop(n, dx, dy, dc):
-        return remote(dsrc, DG.at[me], plane_send, plane_recv.at[n], at(dx, dy, 0, lax.rem(c + dc, 2)))
+        return remote(dsrc.at[0:NP], DG.at[me], plane_send, plane_recv.at[n], at(dx, dy, 0, lax.rem(c + dc, 2)))
 
     def plane_id(dx, dy, dc):
         x, yh, core, yl, _ = at(-dx, -dy, 0, lax.rem(c + dc, 2))
         return (x * 4 + yh * 2 + yl) * 2 + core
 
-    diagonal = lax.broadcasted_iota(jnp.int32, (16, 128), 0) == lax.broadcasted_iota(jnp.int32, (16, 128), 1)
+    diagonal = lax.broadcasted_iota(jnp.int32, (NP, 128), 0) == lax.broadcasted_iota(jnp.int32, (NP, 128), 1)
 
     def to_row(column):
         return jnp.sum(jnp.where(diagonal, column, 0.0), axis=0, keepdims=True)
@@ -374,7 +376,7 @@
     ring(zsrc.at[0], ZA, za_send, za_recv)
     for n, h in enumerate(plane):
         plane_hop(n, *h).start()
-    logdeg_out[...] = (jnp.log(degree) * (1.0 / math.log(10.0)))[0:NP, :]
+    logdeg_out[...] = jnp.log(degree) * (1.0 / math.log(10.0))
     ZA[pl.ds(pz, 1)] = mine[None]
     ring_in(zsrc.at[0], ZA, za_send, za_recv)
     mine = functools.reduce(jnp.maximum, [ZA[k] for k in range(8)])
@@ -383,11 +385,11 @@
         remote(zsrc.at[1], PA.at[me], pa_send, pa_recv.at[n], at(dx, dy, 0, lax.rem(c + dc, 2))).start()
     PA[pl.ds(me, 1)] = mine[None]
     for n, h in enumerate(plane):
-        remote(dsrc, DG.at[plane_id(*h)], plane_send, plane_recv.at[n], partner).wait_recv()
+        remote(dsrc.at[0:NP], DG.at[plane_id(*h)], plane_send, plane_recv.at[n], partner).wait_recv()
     for n, h in enumerate(plane):
         remote(zsrc.at[1], PA.at[plane_id(*h)], pa_send, pa_recv.at[n], partner).wait_recv()
     peak_row = functools.reduce(jnp.maximum, [PA[k] for k in range(32)])
-    peak = jnp.broadcast_to(jnp.sum(jnp.where(diagonal, peak_row, 0.0), axis=1, keepdims=True), (16, 128))
+    peak = jnp.broadcast_to(jnp.sum(jnp.where(diagonal, peak_row, 0.0), axis=1, keepdims=True), (NP, 128))
 
     def weights(k, sums):
         d = DG[k]
@@ -395,9 +397,9 @@
         near = [jnp.maximum(0.0, 1.0 - jnp.abs(position - float(b))) for b in range(BINS)]
         return tuple(s + v for s, v in zip(sums, [*near, d], strict=True))
 
-    sums = lax.fori_loop(0, 32, weights, tuple(jnp.zeros((16, 128), F32) for _ in range(BINS + 1)))
-    lanes = lax.broadcasted_iota(jnp.int32, (16, 128), 1)
-    found = jnp.zeros((16, 128), F32)
+    sums = lax.fori_loop(0, 32, weights, tuple(jnp.zeros((NP, 128), F32) for _ in range(BINS + 1)))
+    lanes = lax.broadcasted_iota(jnp.int32, (NP, 128), 1)
+    found = jnp.zeros((NP, 128), F32)
     for b in range(BINS + 1):
         found = jnp.where(lanes == b, jnp.sum(sums[b], axis=1, keepdims=True), found)
     fsrc[...] = found
@@ -415,7 +417,7 @@
     dev_y = jnp.where(used, fit_y - jnp.sum(fit_y, axis=1, keepdims=True) / BINS, 0.0)
     slope = jnp.sum(dev_x * dev_y, axis=1, keepdims=True) / jnp.sum(dev_x * dev_x, axis=1, keepdims=True)
     mean_log = jnp.log(freq[:, BINS : BINS + 1]) * log10
-    freq_out[...] = freq[0:NP, 0:BINS]
+    freq_out[...] = freq[:, 0:BINS]
     small_out[0:1, :] = to_row(slope)
     small_out[1:2, :] = to_row(mean_log)
 
@@ -452,17 +454,17 @@
             pltpu.VMEM((NS + 1, 2, NP, 8, 128), F32),
             pltpu.VMEM((NS, G, 128), F32),
             pltpu.VMEM((NS, G, 128), F32),
-            pltpu.VMEM((2 * NS, 8, 128), F32),
+            pltpu.VMEM((2 * NS, 4, 128), F32),
             pltpu.VMEM((NS, 2, 16, 128), F32),
-            pltpu.VMEM((2 * NS, 16, 128), F32),
-            pltpu.VMEM((32, 16, 128), F32),
+            pltpu.VMEM((2 * NS, NP, 128), F32),
+            pltpu.VMEM((32, NP, 128), F32),
             pltpu.VMEM((8, 1, 128), F32),
             pltpu.VMEM((32, 1, 128), F32),
-            pltpu.VMEM((8, 16, 128), F32),
-            pltpu.VMEM((8, 128), F32),
-            pltpu.VMEM((16, 128), F32),
+            pltpu.VMEM((8, NP, 128), F32),
+            pltpu.VMEM((4, 128), F32),
+            pltpu.VMEM((NP, 128), F32),
             pltpu.VMEM((2, 1, 128), F32),
-            pltpu.VMEM((16, 128), F32),
+            pltpu.VMEM((NP, 128), F32),
             dma, dma((NS * PIECES,)), dma, dma((NS * PIECES,)), dma, dma((2 * NS,)),
             dma, dma((2 * NS,)), dma, dma((31,)), dma, dma((8,)), dma, dma((31,)), dma, dma((8,)),
         ],

time: 79.4 us -> 78.4 us (0.987)
  Pallas kernels: 76.1 us -> 75.1 us
    pallas_call x1, Pallas kernels: 76.1 us -> 75.1 us  [on_device(): pl.pallas_call(body, out_shape=[jax.ShapeDtypeStruct((NP, G), F32), jax.S...]
where the time goes in v3:
time: 78.4 us; the launch traced here: 78.2 us
  Pallas kernels  75.1 us (96%)
  local copies, waits for them, and re-layouts  2.52 us (3%)
    pallas_call x1, Pallas kernels, on_device(): pl.pallas_call(body, out_shape=[jax.ShapeDtypeStruct((NP, G), F32), jax.S...  75.1 us

profile of v3, /device:TPU:1, one launch (start us, length us, event | category | flops | bytes accessed | tf_op | source)
XLA Modules:
  0.0 78.2 jit_solution(5796887283523756253)
XLA Ops:
  0.6 75.1 %scale_free_fit.1 = (f32[10,128]{1,0:T(8,128)}, f32[10,10]{1,0:T(8,128)}, f32[2,128]{1,0:T(2,128)}) custom-call(s32[10]{0:T(128)} %refs_0_.1, bf16[128,1024]{1,0:T(8,128)(2,1)} %refs_1_.1), custom_call_target="tpu_custom_call" | custom-call | tf_op jit(solution)/shard_map/scale_free_fit/pallas_call | solution.py:441
  75.7 0.0 copy-start.1
  75.7 1.2 %slice_bitcast_fusion = (f32[10]{0:T(128)}, f32[10]{0:T(128)}) fusion(f32[2,128]{1,0:T(2,128)} %get-tuple-element.9), kind=kLoop, calls=%fused_computation | loop fusion | bytes 160 | tf_op jit(solution)/shard_map/squeeze | solution.py:474
  76.9 0.0 copy-done.1
  76.9 0.0 copy-start
  76.9 0.6 copy.8
  77.5 0.1 copy-done
  77.6 0.6 copy.9
Async XLA Ops:
  75.7 1.2 %copy-start.1 = (f32[10,128]{1,0:T(8,128)S(1)}, f32[10,128]{1,0:T(8,128)}, u32[]{:S(2)}) copy-start(f32[10,128]{1,0:T(8,128)} %get-tuple-element.16) | copy-start | bytes 15364
  76.9 0.7 copy-start

commit v4 on v3

--- a/solution.py
+++ b/solution.py
@@ -34,12 +34,12 @@
     (14, 1), (13, 0), (15, 1), (14, 0), (15, 0), (16, 0), (18, 1), (16, 1), (17, 0), (17, 1), (18, 0),
 )
 PAIRS = (
-    (2, 1, 1, 0, 4), (3, 0, 2, 0, 0), (4, 0, 1, 0, 0), (5, 0, 1, 0, 0), (5, 2, 3, 1, 0), (6, 0, 1, 0, 0), (6,
-    2, 5, 0, 0), (7, 1, 6, 0, 0), (8, 0, 1, 0, 0), (8, 2, 3, 0, 0), (8, 5, 7, 0, 0), (9, 2, 8, 0, 0), (10, 2,
-    4, 0, 0), (10, 5, 6, 0, 0), (10, 8, 9, 0, 0), (11, 2, 7, 0, 0), (12, 9, 10, 0, 3), (13, 4, 6, 0, 0), (13,
-    8, 9, 0, 0), (13, 11, 12, 0, 0), (14, 4, 6, 0, 0), (14, 8, 11, 0, 0), (15, 2, 7, 0, 0), (15, 9, 10, 0, 0),
-    (15, 13, 14, 0, 0), (16, 2, 7, 1, 0), (16, 13, 15, 0, 0), (17, 0, 1, 0, 0), (17, 2, 10, 0, 2), (17, 12,
-    14, 2, 0), (18, 0, 4, 0, 0), (18, 6, 8, 0, 0), (18, 11, 12, 0, 1), (18, 15, 17, 0, 1),
+    (2, 0, 1, 0, 0), (3, 1, 2, 0, 0), (4, 0, 1, 0, 0), (4, 2, 3, 0, 0), (5, 2, 3, 1, 0), (6, 1, 2, 0, 0), (6,
+    5, 5, 0, 4), (7, 1, 6, 0, 0), (8, 1, 2, 0, 0), (8, 3, 5, 0, 0), (8, 6, 7, 2, 0), (9, 2, 8, 0, 0), (10, 4,
+    6, 0, 0), (10, 8, 9, 0, 0), (11, 1, 2, 0, 0), (11, 7, 10, 0, 0), (12, 5, 7, 0, 0), (12, 9, 10, 0, 3), (13,
+    4, 6, 0, 0), (13, 8, 9, 0, 0), (13, 11, 12, 0, 0), (14, 4, 6, 0, 0), (14, 8, 11, 0, 0), (15, 2, 7, 0, 0),
+    (15, 10, 12, 0, 0), (15, 13, 14, 0, 0), (16, 2, 7, 1, 0), (16, 12, 15, 0, 0), (17, 2, 7, 0, 0), (17, 10,
+    14, 2, 0), (18, 2, 4, 0, 0), (18, 6, 8, 0, 0), (18, 11, 12, 0, 1), (18, 15, 17, 0, 1),
 )
 STEPS = ((1, 0, 0), (-1, 0, 0), (0, 1, 0), (0, -1, 0), (0, 0, 1), (0, 0, -1))
 NS = len(OFFSETS)
@@ -58,7 +58,7 @@
 
 FIRST = {j: q for i, q, k, j in reversed(HOPS)}
 LEFTS = sorted({0} | {p[1] for p in PAIRS} | {p[2] for p in PAIRS})
-LANES = 128
+EARLY = (15,)
 
 
 def coded(values, width):
@@ -102,7 +102,7 @@
 
 
 def kernel(
-    pw, e, logdeg_out, freq_out, small_out,
+    pw, e, out,
     X, Y, racc, cacc, LM, LI, ST, PS, RB, DG, ZA, PA, ZB, tile, dsrc, zsrc, fsrc,
     piece_send, piece_recv, pair_send, pair_recv, stat_send, stat_recv,
     part_send, part_recv, plane_send, plane_recv, za_send, za_recv, pa_send, pa_recv, zb_send, zb_recv, acc0, acc1,
@@ -295,13 +295,29 @@
             known[0] += 1
             ready(known[0])
 
+    def gather_cols(s, _):
+        for h in range(2):
+            PS[s, h, 0:NP, :] = PS[s, h, 0:NP, :] + jnp.sum(cacc[s, h], axis=1)
+        return 0
+
+    def gather_rows(s):
+        for p in range(NP):
+            sums = jnp.sum(racc[s, p].T.reshape(16, 8, 128), axis=0)
+            PS[s, c, p : p + 1, :] = PS[s, c, p : p + 1, :] + jnp.sum(sums, axis=0, keepdims=True)
+
     stages = sorted({p[0] for p in PAIRS})
+    last_use = {a: max(p[0] for p in PAIRS if a in p[1:3]) for a in LEFTS}
+    gathered = []
     arrive(stages[0])
     arrive(stages[1])
     prepare(stages[0])
     first = next(p for p in PAIRS if p[0] == stages[0])
     multiply(*first[0:3])
     for n, b in enumerate(stages):
+        if stages[min(n + 2, len(stages) - 1)] in EARLY:
+            done = [a for a in LEFTS if last_use[a] < b and a not in gathered]
+            over_list(done, gather_rows)
+            gathered.extend(done)
         arrive(stages[min(n + 2, len(stages) - 1)])
         prepare(stages[min(n + 1, len(stages) - 1)])
         here = [p for p in PAIRS if p[0] == b]
@@ -310,16 +326,6 @@
     pltpu.matmul_pop(acc0)
     pltpu.matmul_pop(acc1)
 
-    def gather_cols(s, _):
-        for h in range(2):
-            PS[s, h, 0:NP, :] = jnp.sum(cacc[s, h], axis=1)
-        return 0
-
-    def gather_rows(s):
-        for p in range(NP):
-            sums = jnp.sum(racc[s, p].T.reshape(16, 8, 128), axis=0)
-            PS[s, c, p : p + 1, :] = PS[s, c, p : p + 1, :] + jnp.sum(sums, axis=0, keepdims=True)
-
     def part(slot, half):
         x, y, z = offset_of(OFFSETS[slot])
         return remote(PS.at[slot, half, 0:NP], RB.at[2 * slot + c], part_send, part_recv.at[2 * slot + c], at(x, y, z, half))
@@ -335,8 +341,8 @@
         return min(x, 4 - x) + min(y, 4 - y) + min(z, 8 - z)
 
     lax.fori_loop(1, NS, gather_cols, 0)
-    send_parts([s for s in range(1, NS) if s not in LEFTS])
-    by_distance = sorted(LEFTS, key=lambda s: -far(s))
+    send_parts([s for s in range(1, NS) if s not in LEFTS or s in gathered])
+    by_distance = sorted((s for s in LEFTS if s not in gathered), key=lambda s: -far(s))
     for k in range(0, len(by_distance), 6):
         over_list(by_distance[k : k + 6], gather_rows)
         send_parts(by_distance[k : k + 6])
@@ -376,7 +382,7 @@
     ring(zsrc.at[0], ZA, za_send, za_recv)
     for n, h in enumerate(plane):
         plane_hop(n, *h).start()
-    logdeg_out[...] = jnp.log(degree) * (1.0 / math.log(10.0))
+    out[0:NP, :] = jnp.log(degree) * (1.0 / math.log(10.0))
     ZA[pl.ds(pz, 1)] = mine[None]
     ring_in(zsrc.at[0], ZA, za_send, za_recv)
     mine = functools.reduce(jnp.maximum, [ZA[k] for k in range(8)])
@@ -417,9 +423,9 @@
     dev_y = jnp.where(used, fit_y - jnp.sum(fit_y, axis=1, keepdims=True) / BINS, 0.0)
     slope = jnp.sum(dev_x * dev_y, axis=1, keepdims=True) / jnp.sum(dev_x * dev_x, axis=1, keepdims=True)
     mean_log = jnp.log(freq[:, BINS : BINS + 1]) * log10
-    freq_out[...] = freq[:, 0:BINS]
-    small_out[0:1, :] = to_row(slope)
-    small_out[1:2, :] = to_row(mean_log)
+    out[16 : 16 + NP, :] = freq
+    out[32:33, :] = to_row(slope)
+    out[33:34, :] = to_row(mean_log)
 
     half_x = X.at[0]
     pltpu.make_async_copy(half_x.at[0 : NS - 1], half_x.at[0 : NS - 1], piece_send).wait()
@@ -438,15 +444,11 @@
     def body(*refs):
         pl.run_scoped(functools.partial(kernel, *refs), pltpu.ACC(0)((2 * G, 256), F32), pltpu.ACC(1)((2 * G, 256), F32))
 
-    logdeg, freq, small = pl.pallas_call(
+    packed = pl.pallas_call(
         body,
-        out_shape=[
-            jax.ShapeDtypeStruct((NP, G), F32),
-            jax.ShapeDtypeStruct((NP, BINS), F32),
-            jax.ShapeDtypeStruct((2, 128), F32),
-        ],
+        out_shape=jax.ShapeDtypeStruct((40, 128), F32),
         in_specs=[pl.BlockSpec(memory_space=pltpu.SMEM), vmem],
-        out_specs=[vmem] * 3,
+        out_specs=vmem,
         scratch_shapes=[
             pltpu.VMEM((2, NS, G, S), jnp.bfloat16),
             pltpu.VMEM((2, G, 2 * G), F32),
@@ -471,7 +473,7 @@
         compiler_params=pltpu.CompilerParams(collective_id=0, has_side_effects=True, vmem_limit_bytes=60 * 2**20),
         name="scale_free_fit",
     )(powers, expression)
-    return (logdeg, freq, small[0, 0:NP], small[1, 0:NP])
+    return (packed[0:NP], packed[16 : 16 + NP, 0:BINS], packed[32, 0:NP], packed[33, 0:NP])
 
 
 def solution(mesh):

time: 78.4 us -> 79.6 us (1.015)
  local copies, waits for them, and re-layouts: 2.52 us -> 3.86 us
    slice x0 -> x2, local copies, waits for them, and re-layouts: none -> 2.59 us  [the longest x1 1.3 us: on_device(): packed[16:16 + NP, 0:BINS]]
    unnamed x6 -> x0, local copies, waits for them, and re-layouts: 1.3 us -> none
where the time goes in v4:
time: 79.6 us; the launch traced here: 79.2 us
  Pallas kernels  74.7 us (94%)
  local copies, waits for them, and re-layouts  3.86 us (5%)
    pallas_call x1, Pallas kernels, on_device(): pl.pallas_call(body, out_shape=jax.ShapeDtypeStruct((40, 128), F32), in_s...  74.7 us

profile of v4, /device:TPU:1, one launch (start us, length us, event | category | flops | bytes accessed | tf_op | source)
XLA Modules:
  0.0 79.2 jit_solution(3877090475973902243)
XLA Ops:
  0.6 74.7 %scale_free_fit.1 = f32[40,128]{1,0:T(8,128)} custom-call(s32[10]{0:T(128)} %refs_0_.1, bf16[128,1024]{1,0:T(8,128)(2,1)} %refs_1_.1), custom_call_target="tpu_custom_call" | custom-call | tf_op jit(solution)/shard_map/scale_free_fit/pallas_call | solution.py:447
  75.4 1.3 %slice_bitcast_fusion = (f32[10]{0:T(128)}, f32[10]{0:T(128)}) fusion(f32[40,128]{1,0:T(8,128)} %scale_free_fit.1), kind=kLoop, calls=%fused_computation | loop fusion | bytes 160 | tf_op jit(solution)/shard_map/squeeze | solution.py:476
  76.6 1.3 %slice.13 = f32[10,10]{1,0:T(8,128)} slice(f32[40,128]{1,0:T(8,128)} %scale_free_fit.1), slice={[16:26], [0:10]} | slice | bytes 800 | tf_op jit(solution)/shard_map/slice | solution.py:476
  77.9 1.3 %slice.12 = f32[10,128]{1,0:T(8,128)} slice(f32[40,128]{1,0:T(8,128)} %scale_free_fit.1), slice={[0:10], [0:128]} | slice | bytes 10240 | tf_op jit(solution)/shard_map/slice | solution.py:476
